TPU v7x, 32 devices: a whole 2x2x4 slice. The times are simulated.
32 devices in a mesh: gx: 2 (over x), gy: 4 (over y, core), gz: 4 (over z).
Axes of the slice: x: 2, y: 2, z: 4, core: 2. Of those that a mesh axis runs over, the one named last changes fastest.
Arguments:
- images: bfloat16 [32, 5, 524288], P(('gx', 'gy', 'gz')), may hold values from 0 to 0.125
- order: int32 [32], replicated, may hold values from 0 to 31, as said below
Outputs:
- frame: float32 [5, 524288], P(None, 'gx')
Inputs may be any that keep to these rules, and one draw needn't show every extreme that they name: order is a permutation of the bricks, where brick r sits at index r // 16 along gx, (r // 4) % 4 along gy and r % 4 along gz; the bricks of one gz index take consecutive places, within them the bricks of one (gy, gz) pair take consecutive places; the order of gz indices, the order of gy indices within each gz index and the order of gx indices within each (gy, gz) pair are arbitrary and may differ from slab to slab and from column to column.
All inputs are finite; a program needn't handle non-finite values.
Results may differ from a plain program's by a relative error of at most 0.0003.
Values may be sent and summed in bfloat16 or wider, within the bound.
A program may use at most 64 MiB of HBM per device.

v0:
```python
import jax
import jax.numpy as jnp
from jax import lax
from jax.sharding import PartitionSpec as P


def composite(stacked, member_keys):
    ranked = jnp.argsort(member_keys)

    def layer(total, member):
        picture = lax.dynamic_index_in_dim(stacked, member, 0, keepdims=False).astype(jnp.float32)
        return (total + (1.0 - total[4:5]) * picture, None)

    start = jnp.zeros(stacked.shape[1:], jnp.float32)
    total, _ = lax.scan(layer, start, ranked)
    return total[None]


def per_device(images, order):
    count_x = lax.axis_size("gx")
    count_y = lax.axis_size("gy")
    count_z = lax.axis_size("gz")
    bricks_all = count_x * count_y * count_z
    place_z = lax.axis_index("gz")
    grid_order = order.reshape(count_x, count_y, count_z)
    column_order = lax.dynamic_index_in_dim(grid_order, place_z, 2, keepdims=False)
    pixels = images.shape[2]
    layers = images.reshape(1, images.shape[1], bricks_all, pixels // bricks_all)
    joined_keys = column_order.reshape(-1)
    partial_value = composite(
        lax.all_to_all(layers, ("gx", "gy"), split_axis=2, concat_axis=0, tiled=True), joined_keys
    )
    slab_keys = jnp.min(grid_order, axis=(0, 1))
    partial_value = composite(
        lax.all_to_all(partial_value, "gz", split_axis=2, concat_axis=0, tiled=True), slab_keys
    )
    tiles = lax.all_gather(partial_value, ("gy", "gz"), axis=2, tiled=True)
    return tiles.reshape(tiles.shape[1], -1)


def solution(mesh):
    in_specs = (P(("gx", "gy", "gz"), None, None), P())
    out_specs = P(None, "gx")
    return jax.shard_map(
        per_device, mesh=mesh, in_specs=in_specs, out_specs=out_specs, check_vma=False
    )
```

profile of v0, /device:TPU:0, one launch (start us, length us, event | category | flops | bytes accessed | tf_op | source)
XLA Modules:
  0.0 295.9 jit_solution(15883542343164375677)
XLA Ops:
  6.5 5.3 %all-to-all-start = ((bf16[1,5,32,16384]{3,1,0,2:T(8,128)(2,1)}), bf16[1,5,32,16384]{3,1,0,2:T(8,128)(2,1)}, u32[]{:S(2)}, u32[]{:S(2)}) async-start(bf16[1,5,32,16384]{3,1,0,2:T(8,128)(2,1)} %bitcast.44), calls=%async_computation | async-start | bytes 16777216 | tf_op jit(solution)/shard_map/all_to_all | solution.py:31
  11.9 0.1 reshape.57
  12.0 0.2 dynamic-slice_reduce_fusion
  12.2 0.1 reshape.58
  12.3 1.0 sort.35
  13.2 92.2 %all-to-all-done = bf16[1,5,32,16384]{3,1,0,2:T(8,128)(2,1)} async-done(((bf16[1,5,32,16384]{3,1,0,2:T(8,128)(2,1)}), bf16[1,5,32,16384]{3,1,0,2:T(8,128)(2,1)}, u32[]{:S(2)}, u32[]{:S(2)}) %all-to-all-start) | async-done | bytes 5242912 | tf_op jit(solution)/shard_map/all_to_all | solution.py:31
  105.4 10.4 %copy.29 = bf16[1,5,8,4,16384]{4,3,1,2,0:T(4,128)(2,1)} copy(bf16[1,5,8,4,16384]{4,1,3,2,0:T(8,128)(2,1)} %bitcast.1) | data formatting | bytes 10485760 | tf_op jit(solution)/shard_map/all_to_all | solution.py:31
  115.8 39.8 %while.22 = (s32[]{:T(128)}, f32[5,4,16384]{2,1,0:T(4,128)S(1)}, s32[8]{0:T(128)S(1)}, bf16[8,5,4,16384]{3,2,1,0:T(4,128)(2,1)}, s32[]{:T(128)}, /*index=5*/s32[]{:T(128)}, s32[]{:T(128)}) while((s32[]{:T(128)}, f32[5,4,16384]{2,1,0:T(4,128)S(1)}, s32[8]{0:T(128)S(1)}, bf16[8,5,4,16384]{3,2,1,0:T(4,128)(2,1)}, s32[]{:T(128)}, ...), condition=%wide.region_4.5_spmd.clone, body=%wide.region_3.4_spmd.clone.sunk | while | flops 1703942 | bytes 6684818 | solution.py:15
  115.8 0.7 dynamic_slice.33
  118.6 0.3 broadcast_select_fusion.4
  118.9 0.1 fusion.6
  118.9 1.8 fusion.7
  120.8 0.7 dynamic_slice.33
  123.5 0.3 broadcast_select_fusion.4
  123.8 0.1 fusion.6
  123.9 1.8 fusion.7
  125.8 0.7 dynamic_slice.33
  128.5 0.3 broadcast_select_fusion.4
  128.8 0.1 fusion.6
  128.9 1.8 fusion.7
  130.7 0.7 dynamic_slice.33
  133.5 0.3 broadcast_select_fusion.4
  133.8 0.1 fusion.6
  133.9 1.8 fusion.7
  135.7 0.7 dynamic_slice.33
  138.5 0.3 broadcast_select_fusion.4
  138.8 0.1 fusion.6
  138.8 1.8 fusion.7
  140.7 0.7 dynamic_slice.33
  143.4 0.3 broadcast_select_fusion.4
  143.7 0.1 fusion.6
  143.8 1.8 fusion.7
  145.7 0.7 dynamic_slice.33
  148.4 0.3 broadcast_select_fusion.4
  148.7 0.1 fusion.6
  148.8 1.8 fusion.7
  150.6 0.7 dynamic_slice.33
  153.4 0.3 broadcast_select_fusion.4
  153.7 0.1 fusion.6
  153.8 1.8 fusion.7
  155.6 2.4 copy.20
  158.0 5.7 %all-to-all-start.1 = ((f32[1,5,4,16384]{3,0,1,2:T(1,128)}), f32[1,5,4,16384]{3,0,1,2:T(1,128)S(1)}, u32[]{:S(2)}, u32[]{:S(2)}) async-start(f32[1,5,4,16384]{3,0,1,2:T(1,128)} %copy.20), calls=%async_computation.1 | async-start | bytes 2621440 | tf_op jit(solution)/shard_map/all_to_all | solution.py:35
  163.7 0.7 sort.34
  164.5 30.3 %all-to-all-done.1 = f32[1,5,4,16384]{3,0,1,2:T(1,128)S(1)} async-done(((f32[1,5,4,16384]{3,0,1,2:T(1,128)}), f32[1,5,4,16384]{3,0,1,2:T(1,128)S(1)}, u32[]{:S(2)}, u32[]{:S(2)}) %all-to-all-start.1) | async-done | bytes 1310752 | tf_op jit(solution)/shard_map/all_to_all | solution.py:35
  194.7 0.8 copy.30
  195.6 14.0 %while.23 = (s32[]{:T(128)}, f32[5,1,16384]{2,1,0:T(1,128)S(1)}, s32[4]{0:T(128)S(1)}, f32[4,5,1,16384]{3,0,1,2:T(4,128)S(1)}, s32[]{:T(128)}, /*index=5*/s32[]{:T(128)}, s32[]{:T(128)}) while((s32[]{:T(128)}, f32[5,1,16384]{2,1,0:T(1,128)S(1)}, s32[4]{0:T(128)S(1)}, f32[4,5,1,16384]{3,0,1,2:T(4,128)S(1)}, s32[]{:T(128)}, ...), condition=%wide.region_6.7_spmd.clone, body=%wide.region_5.6_spmd.clone.sunk | while | flops 344070 | bytes 1835154 | solution.py:15
  195.6 0.6 dynamic_slice.35
  198.1 0.3 broadcast_select_fusion.5
  198.4 0.1 slice_subtract_fusion.3
  198.5 0.6 fusion.8
  199.1 0.6 dynamic_slice.35
  201.6 0.3 broadcast_select_fusion.5
  202.0 0.1 slice_subtract_fusion.3
  202.0 0.6 fusion.8
  202.6 0.6 dynamic_slice.35
  205.1 0.3 broadcast_select_fusion.5
  205.5 0.1 slice_subtract_fusion.3
  205.5 0.6 fusion.8
  206.1 0.6 dynamic_slice.35
  208.7 0.3 broadcast_select_fusion.5
  209.0 0.6 fusion.8
  209.6 1.0 copy.23
  210.7 72.6 %all-gather.3.cloned.1.call-done = f32[5,16,16384]{2,0,1:T(8,128)} async-done(((f32[5,1,16384]{2,0,1:T(8,128)}), f32[5,16,16384]{2,0,1:T(8,128)}) %all-gather.3.cloned.1.call-update) | async-done | bytes 5242896 | tf_op jit(solution)/shard_map/all_gather | solution.py:37
  283.2 5.9 %copy.44 = f32[5,262144]{1,0:T(8,128)} copy(f32[5,262144]{1,0:T(8,128)} %bitcast.45) | data formatting | bytes 10485760
  (10 shorter events, 0.1 us)
Async XLA Ops:
  6.5 5.3 %copy-start = (s32[32]{0:T(128)S(1)}, s32[32]{0:T(128)}, u32[]{:S(2)}) copy-start(s32[32]{0:T(128)} %param.7) | copy-start | bytes 388
  6.5 98.9 %all-to-all-start = ((bf16[1,5,32,16384]{3,1,0,2:T(8,128)(2,1)}), bf16[1,5,32,16384]{3,1,0,2:T(8,128)(2,1)}, u32[]{:S(2)}, u32[]{:S(2)}) async-start(bf16[1,5,32,16384]{3,1,0,2:T(8,128)(2,1)} %bitcast.44), calls=%async_computation | async-start | bytes 16777216 | tf_op jit(solution)/shard_map/all_to_all | solution.py:31
  158.0 36.7 %all-to-all-start.1 = ((f32[1,5,4,16384]{3,0,1,2:T(1,128)}), f32[1,5,4,16384]{3,0,1,2:T(1,128)S(1)}, u32[]{:S(2)}, u32[]{:S(2)}) async-start(f32[1,5,4,16384]{3,0,1,2:T(1,128)} %copy.20), calls=%async_computation.1 | async-start | bytes 2621440 | tf_op jit(solution)/shard_map/all_to_all | solution.py:35
  163.7 119.6 %all-gather.3.cloned.1.call-start = ((), (), s32[]{:S(2)}) async-start(), calls=%async_computation.2 | async-start | bytes 8912896 | tf_op jit(solution)/shard_map/all_gather | solution.py:37
Sparse Core Ops, SparseCore 0:
  210.8 72.4 all-gather.2
where the time goes:
time: 297 us; the launch traced here: 296 us
  waiting for transfers between devices  195 us (66%)
  local copies, waits for them, and re-layouts  28.6 us (10%)
  loops' own time  24.8 us (8%)
  other arithmetic  23.1 us (8%)
  between operations  13.4 us (5%)
  starting transfers between devices  11 us (4%)
    all_to_all x1, waiting for transfers between devices, per_device(): lax.all_to_all(layers, ('gx', 'gy'), split_axis=2, concat_axis=0, tiled=T...  92.2 us
    all_gather x1, waiting for transfers between devices, per_device(): tiles = lax.all_gather(partial_value, ('gy', 'gz'), axis=2, tiled=True)  72.6 us
    all_to_all x1, waiting for transfers between devices, per_device(): lax.all_to_all(partial_value, 'gz', split_axis=2, concat_axis=0, tiled=True)  30.3 us
    another operation x2, loops' own time, composite(): total, _ = lax.scan(layer, start, ranked)  24.8 us
    add x12, other arithmetic, layer(): return (total + (1.0 - total[4:5]) * picture, None)  17 us
    all_to_all x1, local copies, waits for them, and re-layouts, per_device(): lax.all_to_all(layers, ('gx', 'gy'), split_axis=2, concat_axis=0, tiled=T...  10.4 us
    dynamic_slice x12, local copies, waits for them, and re-layouts, composite(): total, _ = lax.scan(layer, start, ranked)  7.7 us
  transfers between devices with their start and end apart: 3, of which 3 were waited for; matrix products, arithmetic and copies ran while one was open for 1% of the time, Pallas kernels for 0%

commit v1 on v0

--- a/solution.py
+++ b/solution.py
@@ -2,6 +2,7 @@
 import jax.numpy as jnp
 from jax import lax
 from jax.sharding import PartitionSpec as P
+from jax.lax import all_gather
 
 
 def composite(stacked, member_keys):
@@ -34,7 +35,8 @@
     partial_value = composite(
         lax.all_to_all(partial_value, "gz", split_axis=2, concat_axis=0, tiled=True), slab_keys
     )
-    tiles = lax.all_gather(partial_value, ("gy", "gz"), axis=2, tiled=True)
+    block_now = all_gather(partial_value, ("gy", "gz"))
+    tiles = jnp.concatenate(block_now, axis=2)
     return tiles.reshape(tiles.shape[1], -1)
 
 

time: 297 us -> 285 us (0.960)
  waiting for transfers between devices: 195 us -> 177 us
  local copies, waits for them, and re-layouts: 28.6 us -> 34.8 us
    all_gather x1, waiting for transfers between devices: 72.6 us -> 54 us  [per_device(): block_now = all_gather(partial_value, ('gy', 'gz'))]
    reshape x0 -> x1, local copies, waits for them, and re-layouts: none -> 5.74 us  [per_device(): tiles = jnp.concatenate(block_now, axis=2)]
    unnamed x3 -> x5, local copies, waits for them, and re-layouts: 5.85 us -> 7.36 us
where the time goes in v1:
time: 285 us; the launch traced here: 284 us
  waiting for transfers between devices  177 us (62%)
  local copies, waits for them, and re-layouts  34.8 us (12%)
  loops' own time  24.8 us (9%)
  other arithmetic  23.1 us (8%)
  between operations  13.4 us (5%)
  starting transfers between devices  11 us (4%)
    all_to_all x1, waiting for transfers between devices, per_device(): lax.all_to_all(layers, ('gx', 'gy'), split_axis=2, concat_axis=0, tiled=T...  92.2 us
    all_gather x1, waiting for transfers between devices, per_device(): block_now = all_gather(partial_value, ('gy', 'gz'))  54 us
    all_to_all x1, waiting for transfers between devices, per_device(): lax.all_to_all(partial_value, 'gz', split_axis=2, concat_axis=0, tiled=True)  30.3 us
    another operation x2, loops' own time, composite(): total, _ = lax.scan(layer, start, ranked)  24.8 us
    add x12, other arithmetic, layer(): return (total + (1.0 - total[4:5]) * picture, None)  17 us
    all_to_all x1, local copies, waits for them, and re-layouts, per_device(): lax.all_to_all(layers, ('gx', 'gy'), split_axis=2, concat_axis=0, tiled=T...  10.4 us
    dynamic_slice x12, local copies, waits for them, and re-layouts, composite(): total, _ = lax.scan(layer, start, ranked)  7.7 us
    unnamed x5, local copies, waits for them, and re-layouts  7.36 us
  transfers between devices with their start and end apart: 3, of which 3 were waited for; matrix products, arithmetic and copies ran while one was open for 1% of the time, Pallas kernels for 0%

profile of v1, /device:TPU:0, one launch (start us, length us, event | category | flops | bytes accessed | tf_op | source)
XLA Modules:
  0.0 283.6 jit_solution(13748867691269585028)
XLA Ops:
  6.5 5.3 %all-to-all-start = ((bf16[1,5,32,16384]{3,1,0,2:T(8,128)(2,1)}), bf16[1,5,32,16384]{3,1,0,2:T(8,128)(2,1)}, u32[]{:S(2)}, u32[]{:S(2)}) async-start(bf16[1,5,32,16384]{3,1,0,2:T(8,128)(2,1)} %bitcast.53), calls=%async_computation | async-start | bytes 16777216 | tf_op jit(solution)/shard_map/all_to_all | solution.py:32
  11.9 0.1 reshape.57
  12.0 0.2 dynamic-slice_reduce_fusion
  12.2 0.1 reshape.58
  12.3 1.0 sort.35
  13.2 92.2 %all-to-all-done = bf16[1,5,32,16384]{3,1,0,2:T(8,128)(2,1)} async-done(((bf16[1,5,32,16384]{3,1,0,2:T(8,128)(2,1)}), bf16[1,5,32,16384]{3,1,0,2:T(8,128)(2,1)}, u32[]{:S(2)}, u32[]{:S(2)}) %all-to-all-start) | async-done | bytes 5242912 | tf_op jit(solution)/shard_map/all_to_all | solution.py:32
  105.4 10.4 %copy.33 = bf16[1,5,8,4,16384]{4,3,1,2,0:T(4,128)(2,1)} copy(bf16[1,5,8,4,16384]{4,1,3,2,0:T(8,128)(2,1)} %bitcast.1) | data formatting | bytes 10485760 | tf_op jit(solution)/shard_map/all_to_all | solution.py:32
  115.8 39.8 %while.22 = (s32[]{:T(128)}, f32[5,4,16384]{2,1,0:T(4,128)S(1)}, s32[8]{0:T(128)S(1)}, bf16[8,5,4,16384]{3,2,1,0:T(4,128)(2,1)}, s32[]{:T(128)}, /*index=5*/s32[]{:T(128)}, s32[]{:T(128)}) while((s32[]{:T(128)}, f32[5,4,16384]{2,1,0:T(4,128)S(1)}, s32[8]{0:T(128)S(1)}, bf16[8,5,4,16384]{3,2,1,0:T(4,128)(2,1)}, s32[]{:T(128)}, ...), condition=%wide.region_4.5_spmd.clone, body=%wide.region_3.4_spmd.clone.sunk | while | flops 1703942 | bytes 6684818 | solution.py:16
  115.8 0.7 dynamic_slice.33
  118.6 0.3 broadcast_select_fusion.4
  118.9 0.1 fusion.6
  118.9 1.8 fusion.7
  120.8 0.7 dynamic_slice.33
  123.5 0.3 broadcast_select_fusion.4
  123.8 0.1 fusion.6
  123.9 1.8 fusion.7
  125.8 0.7 dynamic_slice.33
  128.5 0.3 broadcast_select_fusion.4
  128.8 0.1 fusion.6
  128.9 1.8 fusion.7
  130.7 0.7 dynamic_slice.33
  133.5 0.3 broadcast_select_fusion.4
  133.8 0.1 fusion.6
  133.9 1.8 fusion.7
  135.7 0.7 dynamic_slice.33
  138.5 0.3 broadcast_select_fusion.4
  138.8 0.1 fusion.6
  138.8 1.8 fusion.7
  140.7 0.7 dynamic_slice.33
  143.4 0.3 broadcast_select_fusion.4
  143.7 0.1 fusion.6
  143.8 1.8 fusion.7
  145.7 0.7 dynamic_slice.33
  148.4 0.3 broadcast_select_fusion.4
  148.7 0.1 fusion.6
  148.8 1.8 fusion.7
  150.6 0.7 dynamic_slice.33
  153.4 0.3 broadcast_select_fusion.4
  153.7 0.1 fusion.6
  153.8 1.8 fusion.7
  155.6 2.4 copy.22
  158.0 5.7 %all-to-all-start.1 = ((f32[1,5,4,16384]{3,0,1,2:T(1,128)}), f32[1,5,4,16384]{3,0,1,2:T(1,128)S(1)}, u32[]{:S(2)}, u32[]{:S(2)}) async-start(f32[1,5,4,16384]{3,0,1,2:T(1,128)} %copy.22), calls=%async_computation.1 | async-start | bytes 2621440 | tf_op jit(solution)/shard_map/all_to_all | solution.py:36
  163.7 0.7 sort.34
  164.5 30.3 %all-to-all-done.1 = f32[1,5,4,16384]{3,0,1,2:T(1,128)S(1)} async-done(((f32[1,5,4,16384]{3,0,1,2:T(1,128)}), f32[1,5,4,16384]{3,0,1,2:T(1,128)S(1)}, u32[]{:S(2)}, u32[]{:S(2)}) %all-to-all-start.1) | async-done | bytes 1310752 | tf_op jit(solution)/shard_map/all_to_all | solution.py:36
  194.7 0.8 copy.35
  195.6 14.0 %while.23 = (s32[]{:T(128)}, f32[5,1,16384]{2,1,0:T(1,128)S(1)}, s32[4]{0:T(128)S(1)}, f32[4,5,1,16384]{3,0,1,2:T(4,128)S(1)}, s32[]{:T(128)}, /*index=5*/s32[]{:T(128)}, s32[]{:T(128)}) while((s32[]{:T(128)}, f32[5,1,16384]{2,1,0:T(1,128)S(1)}, s32[4]{0:T(128)S(1)}, f32[4,5,1,16384]{3,0,1,2:T(4,128)S(1)}, s32[]{:T(128)}, ...), condition=%wide.region_6.7_spmd.clone, body=%wide.region_5.6_spmd.clone.sunk | while | flops 344070 | bytes 1835154 | solution.py:16
  195.6 0.6 dynamic_slice.35
  198.1 0.3 broadcast_select_fusion.5
  198.4 0.1 slice_subtract_fusion.3
  198.5 0.6 fusion.8
  199.1 0.6 dynamic_slice.35
  201.6 0.3 broadcast_select_fusion.5
  202.0 0.1 slice_subtract_fusion.3
  202.0 0.6 fusion.8
  202.6 0.6 dynamic_slice.35
  205.1 0.3 broadcast_select_fusion.5
  205.5 0.6 fusion.8
  206.1 0.6 dynamic_slice.35
  208.7 0.3 broadcast_select_fusion.5
  209.0 0.6 fusion.8
  209.6 0.7 copy-done
  210.4 54.0 %all-gather.3.cloned.1.call-done = f32[80,1,16384]{2,1,0:T(1,128)} async-done(((f32[5,1,16384]{2,1,0:T(1,128)}), f32[80,1,16384]{2,1,0:T(1,128)}) %all-gather.3.cloned.1.call-update) | async-done | bytes 5242896 | tf_op jit(solution)/shard_map/all_gather | solution.py:38
  264.4 5.7 %copy.34 = f32[1,5,16,1,16384]{4,2,1,3,0:T(8,128)S(1)} copy(f32[1,5,16,1,16384]{4,3,1,0,2:T(1,128)} %bitcast.56) | data formatting | bytes 10485760 | tf_op jit(solution)/shard_map/reshape | solution.py:39
  270.1 6.6 %copy.29 = f32[1,5,16,16384]{3,1,2,0:T(8,128)} copy(f32[1,5,16,16384]{3,2,1,0:T(8,128)S(1)} %bitcast.51) | data formatting | bytes 10485760
  (12 shorter events, 0.2 us)
Async XLA Ops:
  6.5 5.3 %copy-start.1 = (s32[32]{0:T(128)S(1)}, s32[32]{0:T(128)}, u32[]{:S(2)}) copy-start(s32[32]{0:T(128)} %param.7) | copy-start | bytes 388
  6.5 98.9 %all-to-all-start = ((bf16[1,5,32,16384]{3,1,0,2:T(8,128)(2,1)}), bf16[1,5,32,16384]{3,1,0,2:T(8,128)(2,1)}, u32[]{:S(2)}, u32[]{:S(2)}) async-start(bf16[1,5,32,16384]{3,1,0,2:T(8,128)(2,1)} %bitcast.53), calls=%async_computation | async-start | bytes 16777216 | tf_op jit(solution)/shard_map/all_to_all | solution.py:32
  158.0 36.7 %all-to-all-start.1 = ((f32[1,5,4,16384]{3,0,1,2:T(1,128)}), f32[1,5,4,16384]{3,0,1,2:T(1,128)S(1)}, u32[]{:S(2)}, u32[]{:S(2)}) async-start(f32[1,5,4,16384]{3,0,1,2:T(1,128)} %copy.22), calls=%async_computation.1 | async-start | bytes 2621440 | tf_op jit(solution)/shard_map/all_to_all | solution.py:36
  163.7 100.7 %all-gather.3.cloned.1.call-start = ((), (), s32[]{:S(2)}) async-start(), calls=%async_computation.2 | async-start | bytes 5570560 | tf_op jit(solution)/shard_map/all_gather | solution.py:38
  209.6 0.7 copy-start
Sparse Core Ops, SparseCore 0:
  210.5 53.8 all-gather.2
